TPU v7x, 32 devices: a whole 2x2x4 slice. The times are simulated.
32 devices in a mesh: pairs: 8 (over z, x), stream: 4 (over y, core).
Axes of the slice: x: 2, y: 2, z: 4, core: 2. Of those that a mesh axis runs over, the one named last changes fastest.
Arguments:
- images: bfloat16 [48, 576, 768], P('pairs', 'stream'), may hold values from -6 to 6
- captions: bfloat16 [48, 40, 768], P('pairs', 'stream'), may hold values from -6 to 6
- lengths: int32 [48], P('pairs'), may hold values from 8 to 40
- first_gain: float32 [768], replicated, may hold values from 0.1 to 1.9
- first_shift: float32 [768], replicated, may hold values from -3 to 3
- query_key_value: bfloat16 [768, 2304], replicated, may hold values from -0.21875 to 0.21875
- query_bias: float32 [768], replicated, may hold values from -3 to 3
- value_bias: float32 [768], replicated, may hold values from -3 to 3
- output_weight: bfloat16 [768, 768], replicated, may hold values from -1.25 to 1.25
- output_bias: float32 [768], replicated, may hold values from -3 to 3
- second_gain: float32 [768], replicated, may hold values from 0.1 to 1.9
- second_shift: float32 [768], replicated, may hold values from -3 to 3
- vision_up: bfloat16 [768, 3072], replicated, may hold values from -0.21875 to 0.21875
- vision_up_bias: float32 [3072], replicated, may hold values from -3 to 3
- vision_down: bfloat16 [3072, 768], replicated, may hold values from -0.109375 to 0.109375
- vision_down_bias: float32 [768], replicated, may hold values from -3 to 3
- language_up: bfloat16 [768, 3072], replicated, may hold values from -0.21875 to 0.21875
- language_up_bias: float32 [3072], replicated, may hold values from -3 to 3
- language_down: bfloat16 [3072, 768], replicated, may hold values from -0.109375 to 0.109375
- language_down_bias: float32 [768], replicated, may hold values from -3 to 3
- image_cotangent: bfloat16 [48, 576, 768], P('pairs', 'stream'), may hold values from -6 to 6
- caption_cotangent: bfloat16 [48, 40, 768], P('pairs', 'stream'), may hold values from -6 to 6
Outputs:
- image_out: bfloat16 [48, 576, 768], P('pairs', 'stream')
- caption_out: bfloat16 [48, 40, 768], P('pairs', 'stream')
- image_grad: float32 [48, 576, 768], P('pairs', 'stream')
- caption_grad: float32 [48, 40, 768], P('pairs', 'stream')
- grad_first_gain: float32 [768], replicated
- grad_first_shift: float32 [768], replicated
- grad_query_key_value: float32 [768, 2304], replicated
- grad_query_bias: float32 [768], replicated
- grad_value_bias: float32 [768], replicated
- grad_output_weight: float32 [768, 768], replicated
- grad_output_bias: float32 [768], replicated
- grad_second_gain: float32 [768], replicated
- grad_second_shift: float32 [768], replicated
- grad_vision_up: float32 [768, 3072], P(None, ('pairs', 'stream'))
- grad_vision_up_bias: float32 [3072], replicated
- grad_vision_down: float32 [3072, 768], P(('pairs', 'stream'))
- grad_vision_down_bias: float32 [768], replicated
- grad_language_up: float32 [768, 3072], P(None, ('pairs', 'stream'))
- grad_language_up_bias: float32 [3072], replicated
- grad_language_down: float32 [3072, 768], P(('pairs', 'stream'))
- grad_language_down_bias: float32 [768], replicated
Inputs may be any that keep to these rules, and one draw needn't show every extreme that they name: Caption slots 0 to lengths - 1 of a pair hold its caption; the other slots are padding that no query attends to.
All inputs are finite; a program needn't handle non-finite values.
Results may differ from a plain program's by a relative error of at most 0.013.
The roundings to bfloat16 on the way count: a program that leaves them out, or rounds other values in their place, can miss the bound.
Values may be sent and summed in bfloat16 or wider, within the bound.
No kernel may reach another device: no remote copies, remote signals or barrier semaphores. Data moves between devices by JAX's collectives and lax.ppermute only.
A program may use at most 320 MiB of HBM per device.

v0:
```python
import jax
import jax.numpy as jnp
from jax import lax
from jax.sharding import PartitionSpec as P

HEADS = 12


def standardize(values):
    average = jnp.mean(values, axis=-1, keepdims=True)
    centred = values - average
    inverse = lax.rsqrt(jnp.mean(centred * centred, axis=-1, keepdims=True) + 1e-06)
    return (centred * inverse, inverse)


def norm_backward(upstream, normed, inverse, gain):
    scaled = upstream * gain
    through = (
        scaled
        - jnp.mean(scaled, axis=-1, keepdims=True)
        - normed * jnp.mean(scaled * normed, axis=-1, keepdims=True)
    ) * inverse
    feature_count = upstream.shape[-1]
    gain_grad = jnp.sum((upstream * normed).reshape(-1, feature_count), axis=0)
    shift_grad = jnp.sum(upstream.reshape(-1, feature_count), axis=0)
    return (through, gain_grad, shift_grad)


def exact_gelu(values):
    return jax.nn.gelu(values, approximate=False)


def expert_pass(inputs, cotangent, up_weight, up_bias, down_weight, down_bias):
    hidden = jnp.dot(inputs, up_weight, preferred_element_type=jnp.float32) + up_bias
    activated, gelu_back = jax.vjp(exact_gelu, hidden)
    activated = activated.astype(jnp.bfloat16)
    branch = jnp.dot(activated, down_weight, preferred_element_type=jnp.float32) + down_bias
    down_grad = jnp.einsum("rf,rd->fd", activated, cotangent, preferred_element_type=jnp.float32)
    down_bias_grad = jnp.sum(cotangent.astype(jnp.float32), axis=0)
    act_grad = jnp.einsum("rd,fd->rf", cotangent, down_weight, preferred_element_type=jnp.float32)
    hidden_grad = gelu_back(act_grad)[0].astype(jnp.bfloat16)
    up_grad = jnp.einsum("rd,rf->df", inputs, hidden_grad, preferred_element_type=jnp.float32)
    up_bias_grad = jnp.sum(hidden_grad.astype(jnp.float32), axis=0)
    input_grad = jnp.einsum("rf,df->rd", hidden_grad, up_weight, preferred_element_type=jnp.float32)
    return (branch, input_grad, up_grad, up_bias_grad, down_grad, down_bias_grad)


def attention_scores(queries, key_block, key_valid):
    pair_count, query_rows, width = queries.shape
    query_heads = queries.reshape(pair_count, query_rows, HEADS, width // HEADS)
    key_heads = key_block.reshape(pair_count, key_block.shape[1], HEADS, width // HEADS)
    scores = jnp.einsum(
        "pqhe,pkhe->phqk", query_heads, key_heads, preferred_element_type=jnp.float32
    )
    return jnp.where(key_valid[:, None, None, :], scores, -1e30)


def local(
    images,
    captions,
    lengths,
    first_gain,
    first_shift,
    query_key_value,
    query_bias,
    value_bias,
    output_weight,
    output_bias,
    second_gain,
    second_shift,
    vision_up,
    vision_up_bias,
    vision_down,
    vision_down_bias,
    language_up,
    language_up_bias,
    language_down,
    language_down_bias,
    image_cotangent,
    caption_cotangent,
):
    pair_count, image_rows, width = images.shape
    caption_rows = captions.shape[1]
    local_rows = image_rows + caption_rows
    streams = lax.axis_size("stream")
    head_width = width // HEADS
    sequence = jnp.concatenate([images, captions], axis=1).astype(jnp.float32)
    normed_one, inverse_one = standardize(sequence)
    first = (normed_one * first_gain + first_shift).astype(jnp.bfloat16).reshape(-1, width)
    projected = jnp.dot(first, query_key_value, preferred_element_type=jnp.float32)
    projected = projected.reshape(pair_count, local_rows, 3 * width)
    queries = ((projected[..., :width] + query_bias) * 0.125).astype(jnp.bfloat16)
    key_value_block = jnp.concatenate(
        [projected[..., width : 2 * width], projected[..., 2 * width :] + value_bias], axis=-1
    ).astype(jnp.bfloat16)
    gathered = lax.all_gather(key_value_block, "stream", axis=1, tiled=True)
    key_index = jnp.arange(streams * local_rows, dtype=jnp.int32)
    owner = key_index // local_rows
    within = key_index % local_rows
    text_slot = owner * caption_rows + within - image_rows
    key_valid = (within < image_rows)[None, :] | (text_slot[None, :] < lengths[:, None])
    scores = attention_scores(queries, gathered[..., :width], key_valid)
    row_top = jnp.max(scores, axis=-1, keepdims=True)
    log_total = row_top + jnp.log(jnp.sum(jnp.exp(scores - row_top), axis=-1, keepdims=True))
    weights = jnp.exp(scores - log_total).astype(jnp.bfloat16)
    value_heads = gathered[..., width:].reshape(pair_count, -1, HEADS, head_width)
    mixed = jnp.einsum("phqk,pkhe->pqhe", weights, value_heads, preferred_element_type=jnp.float32)
    mixed = mixed.reshape(pair_count * local_rows, width).astype(jnp.bfloat16)
    middle = sequence + (
        jnp.dot(mixed, output_weight, preferred_element_type=jnp.float32) + output_bias
    ).reshape(pair_count, local_rows, width)
    normed_two, inverse_two = standardize(middle)
    second = (normed_two * second_gain + second_shift).astype(jnp.bfloat16)
    (
        image_branch,
        image_back,
        vision_up_grad,
        vision_up_bias_grad,
        vision_down_grad,
        vision_down_bias_grad,
    ) = expert_pass(
        second[:, :image_rows].reshape(-1, width),
        image_cotangent.reshape(-1, width),
        vision_up,
        vision_up_bias,
        vision_down,
        vision_down_bias,
    )
    (
        caption_branch,
        caption_back,
        language_up_grad,
        language_up_bias_grad,
        language_down_grad,
        language_down_bias_grad,
    ) = expert_pass(
        second[:, image_rows:].reshape(-1, width),
        caption_cotangent.reshape(-1, width),
        language_up,
        language_up_bias,
        language_down,
        language_down_bias,
    )
    image_out = (
        middle[:, :image_rows] + image_branch.reshape(pair_count, image_rows, width)
    ).astype(jnp.bfloat16)
    caption_out = (
        middle[:, image_rows:] + caption_branch.reshape(pair_count, caption_rows, width)
    ).astype(jnp.bfloat16)
    cotangent = jnp.concatenate([image_cotangent, caption_cotangent], axis=1).astype(jnp.float32)
    second_grad = jnp.concatenate(
        [
            image_back.reshape(pair_count, image_rows, width),
            caption_back.reshape(pair_count, caption_rows, width),
        ],
        axis=1,
    )
    through_two, second_gain_grad, second_shift_grad = norm_backward(
        second_grad, normed_two, inverse_two, second_gain
    )
    middle_grad = cotangent + through_two
    branch_grad = middle_grad.astype(jnp.bfloat16).reshape(-1, width)
    output_weight_grad = jnp.einsum(
        "rd,re->de", mixed, branch_grad, preferred_element_type=jnp.float32
    )
    output_bias_grad = jnp.sum(branch_grad.astype(jnp.float32), axis=0)
    mixed_grad = jnp.einsum(
        "re,de->rd", branch_grad, output_weight, preferred_element_type=jnp.float32
    )
    mixed_grad = mixed_grad.astype(jnp.bfloat16).reshape(pair_count, local_rows, HEADS, head_width)
    scores = attention_scores(queries, gathered[..., :width], key_valid)
    probs = jnp.exp(scores - log_total)
    key_heads = gathered[..., :width].reshape(pair_count, -1, HEADS, head_width)
    value_heads = gathered[..., width:].reshape(pair_count, -1, HEADS, head_width)
    query_heads = queries.reshape(pair_count, local_rows, HEADS, head_width)
    prob_grad = jnp.einsum(
        "pqhe,pkhe->phqk", mixed_grad, value_heads, preferred_element_type=jnp.float32
    )
    value_grad = jnp.einsum(
        "phqk,pqhe->pkhe",
        probs.astype(jnp.bfloat16),
        mixed_grad,
        preferred_element_type=jnp.float32,
    )
    score_grad = (probs * (prob_grad - jnp.sum(prob_grad * probs, axis=-1, keepdims=True))).astype(
        jnp.bfloat16
    )
    query_grad = jnp.einsum(
        "phqk,pkhe->pqhe", score_grad, key_heads, preferred_element_type=jnp.float32
    ).astype(jnp.bfloat16)
    key_grad = jnp.einsum(
        "phqk,pqhe->pkhe", score_grad, query_heads, preferred_element_type=jnp.float32
    )
    pair_keys = key_heads.shape[1]
    key_value_grad = jnp.concatenate(
        [
            key_grad.reshape(pair_count, pair_keys, width),
            value_grad.reshape(pair_count, pair_keys, width),
        ],
        axis=-1,
    )
    own_grad = lax.psum_scatter(key_value_grad, "stream", scatter_dimension=1, tiled=True).astype(
        jnp.bfloat16
    )
    projected_grad = jnp.concatenate(
        [query_grad.reshape(pair_count, local_rows, width) * 0.125, own_grad], axis=-1
    ).reshape(-1, 3 * width)
    weight_grad = jnp.einsum("rd,re->de", first, projected_grad, preferred_element_type=jnp.float32)
    query_bias_grad = jnp.sum(projected_grad[:, :width].astype(jnp.float32), axis=0)
    value_bias_grad = jnp.sum(projected_grad[:, 2 * width :].astype(jnp.float32), axis=0)
    first_grad = jnp.einsum(
        "re,de->rd", projected_grad, query_key_value, preferred_element_type=jnp.float32
    )
    first_grad = first_grad.reshape(pair_count, local_rows, width)
    through_one, first_gain_grad, first_shift_grad = norm_backward(
        first_grad, normed_one, inverse_one, first_gain
    )
    input_grad = middle_grad + through_one
    (
        summed_weight,
        summed_output,
        summed_first_gain,
        summed_first_shift,
        summed_query_bias,
        summed_value_bias,
        summed_output_bias,
        summed_second_gain,
        summed_second_shift,
        summed_vision_up_bias,
        summed_vision_down_bias,
        summed_language_up_bias,
        summed_language_down_bias,
    ) = lax.psum(
        (
            weight_grad,
            output_weight_grad,
            first_gain_grad,
            first_shift_grad,
            query_bias_grad,
            value_bias_grad,
            output_bias_grad,
            second_gain_grad,
            second_shift_grad,
            vision_up_bias_grad,
            vision_down_bias_grad,
            language_up_bias_grad,
            language_down_bias_grad,
        ),
        ("pairs", "stream"),
    )
    spread_vision_up, spread_language_up, spread_vision_down, spread_language_down = (
        lax.psum_scatter(vision_up_grad, ("pairs", "stream"), scatter_dimension=1, tiled=True),
        lax.psum_scatter(language_up_grad, ("pairs", "stream"), scatter_dimension=1, tiled=True),
        lax.psum_scatter(vision_down_grad, ("pairs", "stream"), scatter_dimension=0, tiled=True),
        lax.psum_scatter(language_down_grad, ("pairs", "stream"), scatter_dimension=0, tiled=True),
    )
    return (
        image_out,
        caption_out,
        input_grad[:, :image_rows],
        input_grad[:, image_rows:],
        summed_first_gain,
        summed_first_shift,
        summed_weight,
        summed_query_bias,
        summed_value_bias,
        summed_output,
        summed_output_bias,
        summed_second_gain,
        summed_second_shift,
        spread_vision_up,
        summed_vision_up_bias,
        spread_vision_down,
        summed_vision_down_bias,
        spread_language_up,
        summed_language_up_bias,
        spread_language_down,
        summed_language_down_bias,
    )


def solution(mesh):
    placed = (
        P("pairs", "stream", None),
        P("pairs", "stream", None),
        P("pairs"),
        P(),
        P(),
        P(),
        P(),
        P(),
        P(),
        P(),
        P(),
        P(),
        P(),
        P(),
        P(),
        P(),
        P(),
        P(),
        P(),
        P(),
        P("pairs", "stream", None),
        P("pairs", "stream", None),
    )
    return jax.shard_map(
        local,
        mesh=mesh,
        in_specs=placed,
        out_specs=(
            P("pairs", "stream", None),
            P("pairs", "stream", None),
            P("pairs", "stream", None),
            P("pairs", "stream", None),
            P(),
            P(),
            P(),
            P(),
            P(),
            P(),
            P(),
            P(),
            P(),
            P(None, ("pairs", "stream")),
            P(),
            P(("pairs", "stream"), None),
            P(),
            P(None, ("pairs", "stream")),
            P(),
            P(("pairs", "stream"), None),
            P(),
        ),
        check_vma=False,
    )
```

profile of v0, /device:TPU:0, one launch (start us, length us, event | category | flops | bytes accessed | tf_op | source)
XLA Modules:
  0.0 1631.5 jit_solution(4071878750755886414)
XLA Ops:
  12.4 3.9 fusion.7
  19.0 3.5 copy.85
  25.7 3.3 maximum_convert_fusion
  28.9 3.5 reshape.361
  32.5 3.5 fusion.37
  36.0 4.1 reshape.360
  40.1 4.0 copy.87
  45.5 76.4 %all-gather.2.cloned.1.call-done = bf16[6,616,1536]{2,0,1:T(8,128)(2,1)} async-done(((bf16[6,154,1536]{2,0,1:T(8,128)(2,1)}), bf16[6,616,1536]{2,0,1:T(8,128)(2,1)}) %all-gather.2.cloned.1.call-update) | async-done | bytes 11354128 | tf_op jit(solution)/shard_map/all_gather | solution.py:96
  121.9 10.6 fusion.41
  132.6 10.1 copy.105
  142.6 10.0 copy.104
  152.7 18.4 %select_reduce_fusion = (f32[6,12,154]{2,1,0:T(8,128)}, f32[6,12,154,616]{3,2,1,0:T(8,128)}) fusion(pred[6,616]{1,0:T(8,128)(4,1)S(1)} %compare_or_fusion, bf16[6,154,12,64]{1,3,2,0:T(8,128)(2,1)} %bitcast.74, bf16[6,616,12,64]{1,3,2,0:T(8,128)(2,1)} %bitcast.70), kind=kOutput, calls=%fused_computation.4 | convolution fusion | flops 887915968 | bytes 34465200 | tf_op jit(solution)/shard_map/pqhe,pkhe->phqk/dot_general | solution.py:52
  171.0 14.9 exponential_reduce_fusion
  186.0 12.4 convert_bitcast_fusion
  198.4 3.3 copy.89
  201.7 5.8 convert_element_type.115
  207.5 6.5 fusion.40
  217.6 3.3 reshape.346
  220.9 3.8 add_convert_fusion.1
  228.1 3.5 convolution_add_fusion
  231.6 6.7 convert_reduce_fusion.6
  238.4 2.8 fusion.43
  242.9 6.7 fusion.44
  249.6 33.5 %convert_reduce_fusion = (f32[3072]{0:T(1024)}, bf16[864,3072]{1,0:T(8,128)(2,1)S(1)}, f32[864,3072]{1,0:T(8,128)}) fusion(f32[864,3072]{1,0:T(8,128)S(1)} %fusion.44, f32[3072]{0:T(1024)S(1)} %copy-done.51, bf16[864,768]{1,0:T(8,128)(2,1)S(1)} %bitcast.80, bf16[3072,768]{1,0:T(8,128)(2,1)} %param.36), kind=kOutput, calls=%fused_computation.9 | convolution fusion | flops 4275926016 | bytes 32612352 | tf_op jit(solution)/shard_map/rd,fd->rf/dot_general | solution.py:40
  283.1 4.9 fusion.42
  291.2 3.3 concatenate.25
  294.5 4.3 multiply_reduce_fusion.2
  298.9 3.3 convert_reduce_fusion.1
  302.2 2.9 fusion.46
  305.0 2.4 convolution_convert_fusion
  307.5 5.6 reshape.367
  313.1 6.4 copy.93
  319.5 16.9 %fusion.13 = f32[6,12,64,616]{3,2,1,0:T(8,128)} fusion(bf16[6,154,12,64]{1,3,2,0:T(8,128)(2,1)} %copy.93, f32[6,12,154,616]{3,2,1,0:T(8,128)} %get-tuple-element.124, f32[6,12,154]{2,1,0:T(8,128)} %copy-done.23, pred[6,616]{1,0:T(8,128)(4,1)S(1)} %copy-done.27), kind=kOutput, calls=%fused_computation.64 | convolution fusion | flops 894757248 | bytes 40142256 | tf_op jit(solution)/shard_map/phqk,pqhe->pkhe/dot_general | solution.py:179
  336.5 29.1 %multiply_reduce_fusion = (f32[6,12,154]{2,1,0:T(8,128)S(1)}, f32[6,12,154,616]{3,2,1,0:T(8,128)}) fusion(f32[6,12,154,616]{3,2,1,0:T(8,128)} %get-tuple-element.124, f32[6,12,154]{2,1,0:T(8,128)} %copy-done.23, pred[6,616]{1,0:T(8,128)(4,1)S(1)} %copy-done.27, bf16[6,154,12,64]{1,3,2,0:T(8,128)(2,1)} %copy.93, bf16[6,616,12,64]{1,3,2,0:T(8,128)(2,1)} %bitcast.76), kind=kOutput, calls=%fused_computation.1 | convolution fusion | flops 901576384 | bytes 61830384 | tf_op jit(solution)/shard_map/pqhe,pkhe->phqk/dot_general | solution.py:176
  365.5 24.3 %multiply_convert_fusion = bf16[6,12,154,616]{3,2,1,0:T(8,128)(2,1)} fusion(f32[6,12,154,616]{3,2,1,0:T(8,128)} %get-tuple-element.127, f32[6,12,154,616]{3,2,1,0:T(8,128)} %get-tuple-element.124, f32[6,12,154]{2,1,0:T(8,128)S(1)} %get-tuple-element.126, f32[6,12,154]{2,1,0:T(8,128)S(1)} %copy-done.24, pred[6,616]{1,0:T(8,128)(4,1)S(1)} %copy-done.27), kind=kLoop, calls=%fused_computation | loop fusion | flops 34151040 | bytes 68394480 | tf_op jit(solution)/shard_map/convert_element_type | solution.py:185
  389.8 11.1 convert_multiply_fusion
  400.9 12.1 fusion.45
  412.9 13.4 copy.96
  426.3 13.4 copy.95
  439.7 16.5 %pad_maximum_fusion = f32[6,616,1536]{2,1,0:T(8,128)} fusion(f32[6,616,768]{2,1,0:T(8,128)} %copy.96, f32[6,616,768]{2,1,0:T(8,128)} %copy.95), kind=kLoop, calls=%fused_computation.5 | loop fusion | flops 5677056 | bytes 45416448 | tf_op jit(solution)/shard_map/concatenate | solution.py:195
  456.2 385.2 %all-reduce.7 = bf16[6,616,1536]{2,1,0:T(8,128)(2,1)} all-reduce(f32[6,616,1536]{2,1,0:T(8,128)} %pad_maximum_fusion), channel_id=2, replica_groups=mesh['pairs'=8,'stream'=4] {'stream'}, use_global_device_ids=true, to_apply=%region_9.10.clone | all-reduce | flops 5677056 | bytes 34062336
  841.4 3.9 copy.97
  845.4 2.7 dynamic-slice_convert_fusion
  849.8 7.1 convolution_bitcast_fusion
  857.0 6.1 fusion.49
  865.9 6.0 fusion.50
  872.0 9.7 fusion.47
  881.8 9.2 multiply_convert_fusion.1
  893.3 7.7 fusion.48
  906.9 4.7 pad_maximum_fusion.1
  911.6 4.6 reshape.358
  916.2 9.3 multiply_reduce_fusion.3
  928.8 3.4 reshape.359
  932.2 5.8 multiply_add_fusion
  940.5 4.0 convolution_add_fusion.3
  951.0 2.8 convert_reduce_fusion.2
  953.8 42.7 %all-reduce.1 = (f32[768]{0:T(1024)}, f32[768]{0:T(1024)}, f32[768]{0:T(1024)}, f32[768]{0:T(1024)}, f32[768]{0:T(1024)}, /*index=5*/f32[768]{0:T(1024)}, f32[76...) all-reduce(f32[768]{0:T(1024)} %get-tuple-element.86, ...), channel_id=1, replica_groups=mesh['pairs'=8,'stream'=4] {'pairs','stream'}, use_global_device_ids=true, to_apply=%region_13.14 | all-reduce | flops 13056 | bytes 104448 | tf_op jit(solution)/shard_map/psum | solution.py:233
  996.5 7.7 convolution_add_fusion.2
  1005.6 43.7 %all-reduce.6.cloned.1.call-done = (f32[768,2304]{1,0:T(8,128)}, f32[768,768]{1,0:T(8,128)}) async-done(((f32[768,2304]{1,0:T(8,128)}, f32[768,768]{1,0:T(8,128)}), (f32[768,2304]{1,0:T(8,128)}, f32[768,768]{1,0:T(8,128)})) %all-reduce.6.cloned.1.call-update) | async-done | bytes 9437200 | tf_op jit(solution)/shard_map/psum | solution.py:233
  1049.3 142.8 %reduce-scatter.10.cloned.1.call-done = f32[768,96]{0,1:T(8,128)} async-done(((f32[768,3072]{0,1:T(8,128)}), f32[768,96]{0,1:T(8,128)}) %reduce-scatter.10.cloned.1.call-update) | async-done | bytes 294928 | tf_op jit(solution)/shard_map/reduce_scatter | solution.py:253
  1192.0 141.5 %reduce-scatter.12.cloned.1.call-done = f32[96,768]{1,0:T(8,128)} async-done(((f32[3072,768]{1,0:T(8,128)}), f32[96,768]{1,0:T(8,128)}) %reduce-scatter.12.cloned.1.call-update) | async-done | bytes 294928 | tf_op jit(solution)/shard_map/reduce_scatter | solution.py:255
  1333.5 141.5 %reduce-scatter.6.cloned.1.call-done = f32[768,96]{0,1:T(8,128)} async-done(((f32[768,3072]{0,1:T(8,128)}), f32[768,96]{0,1:T(8,128)}) %reduce-scatter.6.cloned.1.call-update) | async-done | bytes 294928 | tf_op jit(solution)/shard_map/reduce_scatter | solution.py:252
  1475.0 141.5 %reduce-scatter.8.cloned.1.call-done = f32[96,768]{1,0:T(8,128)} async-done(((f32[3072,768]{1,0:T(8,128)}), f32[96,768]{1,0:T(8,128)}) %reduce-scatter.8.cloned.1.call-update) | async-done | bytes 294928 | tf_op jit(solution)/shard_map/reduce_scatter | solution.py:254
  1616.5 6.6 copy.110
  (194 shorter events, 51.2 us)
Async XLA Ops:
  7.2 5.2 copy-start
  7.2 5.2 copy-start.54
  7.2 5.2 copy-start.59
  7.2 114.7 %all-gather.2.cloned.1.call-start = ((), (), s32[]{:S(2)}) async-start(), calls=%async_computation.4 | async-start | bytes 18923520 | tf_op jit(solution)/shard_map/all_gather | solution.py:96
  7.3 5.1 copy-start.2
  8.4 7.9 copy-start.15
  10.4 5.9 copy-start.31
  12.4 3.9 copy-start.39
  22.5 1026.8 %all-reduce.6.cloned.1.call-start = ((), (), s32[]{:S(2)}) async-start(), calls=%async_computation.9 | async-start | bytes 18874368 | tf_op jit(solution)/shard_map/psum | solution.py:233
  40.1 4.1 copy-start.61
  40.1 5.3 copy-start.58
  45.5 140.4 %copy-start.26 = (pred[6,616]{1,0:T(8,128)(4,1)}, pred[6,616]{1,0:T(8,128)(4,1)S(1)}, u32[]{:S(2)}) copy-start(pred[6,616]{1,0:T(8,128)(4,1)S(1)} %compare_or_fusion) | copy-start | bytes 11092
  171.0 14.9 copy-start.29
  171.0 14.9 copy-start.7
  185.9 12.5 copy-start.23
  201.7 5.8 copy-start.45
  214.1 6.8 copy-start.38
  216.9 4.0 copy-start.33
  216.9 7.8 copy-start.42
  224.7 3.4 copy-start.50
  228.1 3.5 copy-start.30
  228.1 10.2 slice-start
  231.6 6.8 copy-start.20
  231.6 6.8 slice-start.1
  238.4 2.8 copy-start.25
  242.9 6.7 copy-start.8
  242.9 6.7 copy-start.51
  242.9 40.2 %slice-start.2 = ((s8[4718592]{0:T(1024)(128)(4,1)}), s8[4194304]{0:T(1024)(128)(4,1)S(1)}, s32[]{:S(2)}) async-start(s8[4718592]{0:T(1024)(128)(4,1)} %bitcast.88), calls=%async_computation.12 | async-start | bytes 8388608
  249.5 33.5 %copy-start.13 = (f32[864,3072]{1,0:T(8,128)}, f32[864,3072]{1,0:T(8,128)S(1)}, u32[]{:S(2)}) copy-start(f32[864,3072]{1,0:T(8,128)S(1)} %fusion.44) | copy-start | bytes 31850500
  249.6 33.5 %slice-start.3 = ((s8[4718592]{0:T(1024)(128)(4,1)}), s8[524288]{0:T(1024)(128)(4,1)S(1)}, s32[]{:S(2)}) async-start(s8[4718592]{0:T(1024)(128)(4,1)} %bitcast.88), calls=%async_computation.13 | async-start | bytes 1048576
  283.1 5.0 copy-start.62
  283.1 4.9 copy-start.21
  283.1 4.9 copy-start.34
  290.5 4.0 copy-start.37
  290.5 8.3 copy-start.41
  294.5 4.3 copy-start.1
  294.5 4.4 copy-start.6
  294.5 4.4 copy-start.43
  294.5 4.4 copy-start.47
  298.8 3.3 copy-start.44
  298.8 3.3 copy-start.10
  302.2 2.9 copy-start.28
  313.1 6.4 copy-start.27
  336.5 29.1 %copy-start.24 = (f32[6,12,154]{2,1,0:T(8,128)S(1)}, f32[6,12,154]{2,1,0:T(8,128)}, u32[]{:S(2)}) copy-start(f32[6,12,154]{2,1,0:T(8,128)} %copy-done.23) | copy-start | bytes 133060
  389.8 11.1 copy-start.5
  845.3 4.4 copy-start.3
  845.3 4.4 copy-start.14
  845.3 4.4 copy-start.16
  845.3 4.4 copy-start.32
  845.4 4.4 copy-start.40
  845.4 4.4 copy-start.55
  845.4 4.4 copy-start.60
  856.9 335.1 %reduce-scatter.10.cloned.1.call-start = ((), (), s32[]{:S(2)}) async-start(), calls=%async_computation.7 | async-start | bytes 9732096 | tf_op jit(solution)/shard_map/reduce_scatter | solution.py:253
  863.2 470.3 %reduce-scatter.12.cloned.1.call-start = ((), (), s32[]{:S(2)}) async-start(), calls=%async_computation.8 | async-start | bytes 9732096 | tf_op jit(solution)/shard_map/reduce_scatter | solution.py:255
  871.9 603.1 %reduce-scatter.6.cloned.1.call-start = ((), (), s32[]{:S(2)}) async-start(), calls=%async_computation.5 | async-start | bytes 9732096 | tf_op jit(solution)/shard_map/reduce_scatter | solution.py:252
  881.7 734.8 %reduce-scatter.8.cloned.1.call-start = ((), (), s32[]{:S(2)}) async-start(), calls=%async_computation.6 | async-start | bytes 9732096 | tf_op jit(solution)/shard_map/reduce_scatter | solution.py:254
  881.8 11.6 copy-start.9
  911.6 4.6 copy-start.56
  925.5 6.7 copy-start.35
  940.5 9.2 copy-start.46
  944.4 9.4 copy-start.48
  944.4 9.4 copy-start.49
  996.5 7.8 copy-start.4
  1616.5 6.6 copy-start.22
  (9 other events, 13.9 us)
Sparse Core Ops, SparseCore 0:
  22.6 99.3 all-gather.1
  857.1 192.1 all-reduce.5
  1055.7 136.2 reduce-scatter.9
  1198.4 135.1 reduce-scatter.11
  1339.8 135.1 reduce-scatter.5
  1481.3 135.1 reduce-scatter.7
where the time goes:
time: 1640 us; the launch traced here: 1630 us
  waiting for transfers between devices  687 us (42%)
  blocking collectives  428 us (26%)
  matrix products  231 us (14%)
  local copies, waits for them, and re-layouts  153 us (9%)
  other arithmetic  116 us (7%)
    unnamed x1, blocking collectives  385 us
    reduce_scatter x1, waiting for transfers between devices, local(): lax.psum_scatter(language_up_grad, ('pairs', 'stream'), scatter_dimension...  143 us
    reduce_scatter x1, waiting for transfers between devices, local(): lax.psum_scatter(vision_up_grad, ('pairs', 'stream'), scatter_dimension=1...  142 us
    reduce_scatter x1, waiting for transfers between devices, local(): lax.psum_scatter(vision_down_grad, ('pairs', 'stream'), scatter_dimension...  141 us
    reduce_scatter x1, waiting for transfers between devices, local(): lax.psum_scatter(language_down_grad, ('pairs', 'stream'), scatter_dimensi...  141 us
    all_gather x1, waiting for transfers between devices, local(): gathered = lax.all_gather(key_value_block, 'stream', axis=1, tiled=True)  76.4 us
    psum x1, waiting for transfers between devices, local(): lax.psum((weight_grad, output_weight_grad, first_gain_grad, first_shift_g...  43.7 us
    psum x1, blocking collectives, local(): lax.psum((weight_grad, output_weight_grad, first_gain_grad, first_shift_g...  42.7 us
  transfers between devices with their start and end apart: 6, of which 6 were waited for; matrix products, arithmetic and copies ran while one was open for 8% of the time, Pallas kernels for 0%

commit v1 on v0

v1 whole, which is shorter than its diff:
```python
import functools

import jax
import jax.numpy as jnp
from jax import lax
from jax.experimental import pallas as pl
from jax.experimental.pallas import tpu as pltpu
from jax.sharding import PartitionSpec as P

HEADS = 12
GROUP = 4
F32 = jnp.float32
BF16 = jnp.bfloat16
VMEM_LIMIT = 63 * 1024 * 1024
BOTH = ("pairs", "stream")


def params(steps):
    return pltpu.CompilerParams(
        dimension_semantics=("arbitrary",) * steps, vmem_limit_bytes=VMEM_LIMIT
    )


def whole(shape):
    return pl.BlockSpec(shape, lambda *_: (0,) * len(shape), pipeline_mode=pl.Buffered(1))


def mm(a, b):
    return jnp.dot(a, b, preferred_element_type=F32)


def mm_t(a, b):
    return lax.dot_general(a, b, (((1,), (1,)), ((), ())), preferred_element_type=F32)


def t_mm(a, b):
    return lax.dot_general(a, b, (((0,), (0,)), ((), ())), preferred_element_type=F32)


def standardize(values):
    centred = values - jnp.mean(values, axis=-1, keepdims=True)
    inverse = lax.rsqrt(jnp.mean(centred * centred, axis=-1, keepdims=True) + 1e-06)
    return centred * inverse, inverse


def norm_through(upstream, normed, inverse, gain):
    scaled = upstream * gain
    return (
        scaled
        - jnp.mean(scaled, axis=-1, keepdims=True)
        - normed * jnp.mean(scaled * normed, axis=-1, keepdims=True)
    ) * inverse


def column_sum(values):
    return jnp.sum(values, axis=0, keepdims=True)


def project_kernel(own, far, cap, vec, weight, query, key, value):
    width = own.shape[-1]
    rows = jnp.concatenate([own[0], far[0], cap[0]], axis=0).astype(F32)
    normed, _ = standardize(rows)
    first = (normed * vec[0:1] + vec[1:2]).astype(BF16)
    key[0] = mm(first, weight[:, width : 2 * width]).astype(BF16)
    value[0] = (mm(first, weight[:, 2 * width :]) + vec[3:4]).astype(BF16)
    query[0] = ((mm(first, weight[:, :width]) + vec[2:3]) * 0.125).astype(BF16)


def project(own, far, cap, vec, weight):
    pairs, part, width = own.shape
    rows = 2 * part + cap.shape[1]
    block = lambda n: pl.BlockSpec((1, n, width), lambda i: (i, 0, 0))
    shape = jax.ShapeDtypeStruct((pairs, rows, width), BF16)
    return pl.pallas_call(
        project_kernel,
        grid=(pairs,),
        in_specs=[block(part), block(part), block(cap.shape[1]), whole(vec.shape), whole(weight.shape)],
        out_specs=[block(rows)] * 3,
        out_shape=[shape] * 3,
        compiler_params=params(1),
        name="project",
        cost_estimate=pl.CostEstimate(
            flops=6 * pairs * rows * width * width, transcendentals=0, bytes_accessed=12_000_000
        ),
    )(own, far, cap, vec, weight)


def stack_heads(values, lanes):
    head = values.shape[-1] // GROUP
    zero = jnp.zeros_like(values)
    return jnp.concatenate(
        [jnp.where(lanes // head == h, values, zero) for h in range(GROUP)], axis=0
    )


def attend_kernel(
    query, key0, value0, key1, value1, bias, own, far, cap, vec, weight,
    mixed, total, mid_own, mid_far, mid_cap, sec_own, sec_far, sec_cap,
    scores, probs,
):
    step = pl.program_id(1)
    rows, span = query.shape[1], query.shape[2]
    part = own.shape[1]
    lanes = lax.broadcasted_iota(jnp.int32, (1, span), 1)
    keys = jnp.concatenate([key0[0], key1[0]], axis=0)
    values = jnp.concatenate([value0[0], value1[0]], axis=0)
    scores[...] = mm_t(stack_heads(query[0], lanes), keys)
    marks = lax.broadcasted_iota(jnp.int32, (1, total.shape[2]), 1)

    @pl.when(step == 0)
    def _():
        total[0] = jnp.zeros(total.shape[1:], F32)

    for h in range(GROUP):
        at = pl.ds(h * rows, rows)
        masked = scores[at] + bias[0]
        top = jnp.max(masked, axis=-1, keepdims=True)
        shifted = jnp.exp(masked - top)
        amount = jnp.sum(shifted, axis=-1, keepdims=True)
        probs[at] = (shifted * (1.0 / amount)).astype(BF16)
        total[0] = jnp.where(marks == step * GROUP + h, top + jnp.log(amount), total[0])
    head = span // GROUP
    result = jnp.zeros((rows, span), F32)
    for h in range(GROUP):
        result = jnp.where(lanes // head == h, mm(probs[pl.ds(h * rows, rows)], values), result)
    mixed[0, :, pl.ds(pl.multiple_of(step * span, span), span)] = result.astype(BF16)

    @pl.when(step == pl.num_programs(1) - 1)
    def _():
        branch = mm(mixed[0], weight[...]) + vec[4:5]
        for place, source, mid, second in (
            (0, own, mid_own, sec_own),
            (part, far, mid_far, sec_far),
            (2 * part, cap, mid_cap, sec_cap),
        ):
            count = source.shape[1]
            middle = source[0].astype(F32) + branch[place : place + count]
            mid[0] = middle
            normed, _ = standardize(middle)
            second[0] = (normed * vec[5:6] + vec[6:7]).astype(BF16)


def attend(query, key0, value0, key1, value1, bias, own, far, cap, vec, weight):
    pairs, rows, width = query.shape
    part, slots = own.shape[1], cap.shape[1]
    span = GROUP * (width // HEADS)
    keys = 2 * rows
    wide = pl.BlockSpec((1, rows, span), lambda i, j: (i, 0, j))
    block = lambda n, w=width: pl.BlockSpec((1, n, w), lambda i, j: (i, 0, 0))
    shape = lambda n, t: jax.ShapeDtypeStruct((pairs, n, width), t)
    return pl.pallas_call(
        attend_kernel,
        grid=(pairs, width // span),
        in_specs=[wide] * 5
        + [block(1, keys), block(part), block(part), block(slots), whole(vec.shape), whole(weight.shape)],
        out_specs=[block(rows), block(rows, 128)] + [block(part), block(part), block(slots)] * 2,
        out_shape=[
            shape(rows, BF16),
            jax.ShapeDtypeStruct((pairs, rows, 128), F32),
            shape(part, F32),
            shape(part, F32),
            shape(slots, F32),
            shape(part, BF16),
            shape(part, BF16),
            shape(slots, BF16),
        ],
        scratch_shapes=[
            pltpu.VMEM((GROUP * rows, keys), F32),
            pltpu.VMEM((GROUP * rows, keys), BF16),
        ],
        compiler_params=params(2),
        name="attend",
        cost_estimate=pl.CostEstimate(
            flops=20_000_000_000, transcendentals=pairs * HEADS * rows * keys, bytes_accessed=20_000_000
        ),
    )(query, key0, value0, key1, value1, bias, own, far, cap, vec, weight)


def expert_kernel(parts, with_weights, block_rows, gain_row, bias_row, *refs):
    refs = list(refs)
    take = lambda n: [refs.pop(0) for _ in range(n)]
    second_in, cotangent_in, middle_in = take(parts), take(parts), take(parts)
    vec, up, up_bias, down = take(4)
    out, back = take(parts), take(parts)
    (up_bias_grad,) = take(1)
    (sums,) = take(1)
    weight_grad = take(1)[0] if with_weights else None
    second, cotangent, hidden, active_grad, active, hidden_grad, branch, second_grad = take(8)
    step = pl.program_id(0)
    count = second_in[0].shape[0]
    width = second.shape[1]

    @pl.when(step == 0)
    def _():
        for i in range(parts):
            second[pl.ds(i * count, count)] = second_in[i][...]
            cotangent[pl.ds(i * count, count)] = cotangent_in[i][...]
        branch[...] = jnp.zeros_like(branch)
        second_grad[...] = jnp.zeros_like(second_grad)

    hidden[...] = mm(second[...], up[...])
    active_grad[...] = mm_t(cotangent[...], down[...])

    def pointwise(i, bias_grad):
        at = pl.ds(pl.multiple_of(i * block_rows, block_rows), block_rows)
        values = hidden[at] + up_bias[...]
        share = 0.5 * (1.0 + lax.erf(values * 0.7071067811865476))
        density = jnp.exp(values * values * -0.5) * 0.3989422804014327
        active[at] = (values * share).astype(BF16)
        grad = (active_grad[at] * (share + values * density)).astype(BF16)
        hidden_grad[at] = grad
        return bias_grad + column_sum(grad.astype(F32))

    rows = parts * count
    up_bias_grad[...] = lax.fori_loop(
        0, rows // block_rows, pointwise, jnp.zeros(up_bias_grad.shape, F32)
    )
    branch[...] += mm(active[...], down[...])
    second_grad[...] += mm_t(hidden_grad[...], up[...])
    if with_weights:
        weight_grad[:, :width] = t_mm(hidden_grad[...], second[...]).astype(BF16)
        weight_grad[:, width:] = t_mm(active[...], cotangent[...]).astype(BF16)

    @pl.when(step == pl.num_programs(0) - 1)
    def _():
        zero = jnp.zeros((1, width), F32)
        sums_now = (zero, zero, zero)
        for i in range(parts):

            def finish(j, carried, i=i):
                at = pl.ds(pl.multiple_of(j * block_rows, block_rows), block_rows)
                all_at = pl.ds(pl.multiple_of(i * count + j * block_rows, 16), block_rows)
                middle = middle_in[i][at]
                out[i][at] = (middle + branch[all_at] + vec[bias_row : bias_row + 1]).astype(BF16)
                normed, inverse = standardize(middle)
                grad = second_grad[all_at]
                cot = cotangent[all_at].astype(F32)
                back[i][at] = cot + norm_through(grad, normed, inverse, vec[gain_row : gain_row + 1])
                gain_sum, shift_sum, cot_sum = carried
                return (
                    gain_sum + column_sum(grad * normed),
                    shift_sum + column_sum(grad),
                    cot_sum + column_sum(cot),
                )

            sums_now = lax.fori_loop(0, count // block_rows, finish, sums_now)
        sums[...] = jnp.concatenate(sums_now + (jnp.zeros((5, width), F32),), axis=0)


def expert(seconds, cotangents, middles, vec, up, up_bias, down, chunk, block_rows, bias_row, with_weights):
    parts = len(seconds)
    count, width = seconds[0].shape
    units = up.shape[1]
    rows = parts * count
    full = whole((count, width))
    resident = pl.BlockSpec((count, width), lambda j: (0, 0))
    shape = lambda t: jax.ShapeDtypeStruct((count, width), t)
    out_specs = [resident] * (2 * parts) + [
        pl.BlockSpec((1, chunk), lambda j: (0, j)),
        pl.BlockSpec((8, width), lambda j: (0, 0)),
    ]
    out_shape = [shape(BF16)] * parts + [shape(F32)] * parts + [
        jax.ShapeDtypeStruct((1, units), F32),
        jax.ShapeDtypeStruct((8, width), F32),
    ]
    if with_weights:
        out_specs.append(pl.BlockSpec((chunk, 2 * width), lambda j: (j, 0)))
        out_shape.append(jax.ShapeDtypeStruct((units, 2 * width), BF16))
    result = pl.pallas_call(
        functools.partial(expert_kernel, parts, with_weights, block_rows, 5, bias_row),
        grid=(units // chunk,),
        in_specs=[full] * (3 * parts)
        + [
            whole(vec.shape),
            pl.BlockSpec((width, chunk), lambda j: (0, j)),
            pl.BlockSpec((1, chunk), lambda j: (0, j)),
            pl.BlockSpec((chunk, width), lambda j: (j, 0)),
        ],
        out_specs=out_specs,
        out_shape=out_shape,
        scratch_shapes=[
            pltpu.VMEM((rows, width), BF16),
            pltpu.VMEM((rows, width), BF16),
            pltpu.VMEM((rows, chunk), F32),
            pltpu.VMEM((rows, chunk), F32),
            pltpu.VMEM((rows, chunk), BF16),
            pltpu.VMEM((rows, chunk), BF16),
            pltpu.VMEM((rows, width), F32),
            pltpu.VMEM((rows, width), F32),
        ],
        compiler_params=params(1),
        name="expert_weights" if with_weights else "expert",
        cost_estimate=pl.CostEstimate(
            flops=(12 if with_weights else 8) * rows * width * units,
            transcendentals=2 * rows * units,
            bytes_accessed=30_000_000,
        ),
    )(*seconds, *cotangents, *middles, vec, up, up_bias, down)
    return result[:parts], result[parts : 2 * parts], *result[2 * parts :]


def share_kernel(second, cotangent, up, up_bias, down, up_grad, down_grad):
    values = mm(second[...], up[...]) + up_bias[...]
    share = 0.5 * (1.0 + lax.erf(values * 0.7071067811865476))
    density = jnp.exp(values * values * -0.5) * 0.3989422804014327
    active = (values * share).astype(BF16)
    active_grad = mm_t(cotangent[...], down[...])
    hidden_grad = (active_grad * (share + values * density)).astype(BF16)

    @pl.when(pl.program_id(0) == 0)
    def _():
        up_grad[...] = jnp.zeros_like(up_grad)
        down_grad[...] = jnp.zeros_like(down_grad)

    up_grad[...] += t_mm(second[...], hidden_grad)
    down_grad[...] += t_mm(active, cotangent[...])


def share_grads(second, cotangent, up, up_bias, down):
    rows, width = second.shape
    units = up.shape[1]
    block_rows = 1024
    tokens = pl.BlockSpec((block_rows, width), lambda i: (i, 0))
    return pl.pallas_call(
        share_kernel,
        grid=(rows // block_rows,),
        in_specs=[tokens, tokens, whole(up.shape), whole(up_bias.shape), whole(down.shape)],
        out_specs=[
            pl.BlockSpec((width, units), lambda i: (0, 0)),
            pl.BlockSpec((units, width), lambda i: (0, 0)),
        ],
        out_shape=[
            jax.ShapeDtypeStruct((width, units), F32),
            jax.ShapeDtypeStruct((units, width), F32),
        ],
        compiler_params=params(1),
        name="share_grads",
        cost_estimate=pl.CostEstimate(
            flops=8 * rows * width * max(units, 128), transcendentals=0, bytes_accessed=7_000_000
        ),
    )(second, cotangent, up, up_bias, down)


def attend_back_kernel(
    grad_own, grad_far, grad_cap, query, key0, value0, key1, value1, bias, mixed, total, weight,
    query_grad, key_grad0, value_grad0, key_grad1, value_grad1, weight_grad, bias_grad,
    mixed_grad, scores, prob_grad, probs, score_grad, weight_sum,
):
    pair, step = pl.program_id(0), pl.program_id(1)
    rows, span = query.shape[1], query.shape[2]
    lanes = lax.broadcasted_iota(jnp.int32, (1, span), 1)

    @pl.when(jnp.logical_and(pair == 0, step == 0))
    def _():
        weight_sum[...] = jnp.zeros_like(weight_sum)
        bias_grad[...] = jnp.zeros_like(bias_grad)

    @pl.when(step == 0)
    def _():
        branch = jnp.concatenate([grad_own[0], grad_far[0], grad_cap[0]], axis=0).astype(BF16)
        mixed_grad[...] = mm_t(branch, weight[...]).astype(BF16)
        weight_sum[...] += t_mm(mixed[0], branch)
        bias_grad[0:1] += column_sum(branch.astype(F32))

    keys = jnp.concatenate([key0[0], key1[0]], axis=0)
    values = jnp.concatenate([value0[0], value1[0]], axis=0)
    queries = stack_heads(query[0], lanes)
    upstream = stack_heads(
        mixed_grad[:, pl.ds(pl.multiple_of(step * span, span), span)], lanes
    )
    scores[...] = mm_t(queries, keys)
    prob_grad[...] = mm_t(upstream, values)
    marks = lax.broadcasted_iota(jnp.int32, (1, total.shape[2]), 1)
    for h in range(GROUP):
        at = pl.ds(h * rows, rows)
        log_total = jnp.sum(
            jnp.where(marks == step * GROUP + h, total[0], 0.0), axis=-1, keepdims=True
        )
        prob = jnp.exp(scores[at] + bias[0] - log_total)
        grad = prob_grad[at]
        centre = jnp.sum(grad * prob, axis=-1, keepdims=True)
        probs[at] = prob.astype(BF16)
        score_grad[at] = (prob * (grad - centre)).astype(BF16)
    head = span // GROUP
    result = jnp.zeros((rows, span), F32)
    for h in range(GROUP):
        result = jnp.where(lanes // head == h, mm(score_grad[pl.ds(h * rows, rows)], keys), result)
    query_grad[0] = (result.astype(BF16).astype(F32) * 0.125).astype(BF16)
    key_grad = t_mm(score_grad[...], queries)
    key_grad0[0] = key_grad[:rows]
    key_grad1[0] = key_grad[rows:].astype(BF16)
    value_grad = t_mm(probs[...], upstream)
    value_grad0[0] = value_grad[:rows]
    value_grad1[0] = value_grad[rows:].astype(BF16)

    @pl.when(jnp.logical_and(pair == pl.num_programs(0) - 1, step == pl.num_programs(1) - 1))
    def _():
        weight_grad[...] = weight_sum[...].astype(BF16)


def attend_back(grads, query, key0, value0, key1, value1, bias, mixed, total, weight):
    pairs, rows, width = query.shape
    part, slots = grads[0].shape[1], grads[2].shape[1]
    span = GROUP * (width // HEADS)
    keys = 2 * rows
    wide = pl.BlockSpec((1, rows, span), lambda i, j: (i, 0, j))
    block = lambda n, w=width: pl.BlockSpec((1, n, w), lambda i, j: (i, 0, 0))
    shape = lambda t: jax.ShapeDtypeStruct((pairs, rows, width), t)
    fixed = lambda s: pl.BlockSpec(s, lambda i, j: (0, 0))
    return pl.pallas_call(
        attend_back_kernel,
        grid=(pairs, width // span),
        in_specs=[block(part), block(part), block(slots)]
        + [wide] * 5
        + [block(1, keys), block(rows), block(rows, 128), whole(weight.shape)],
        out_specs=[wide] * 5 + [fixed((width, width)), fixed((8, width))],
        out_shape=[shape(BF16), shape(F32), shape(F32), shape(BF16), shape(BF16)]
        + [jax.ShapeDtypeStruct((width, width), BF16), jax.ShapeDtypeStruct((8, width), F32)],
        scratch_shapes=[
            pltpu.VMEM((rows, width), BF16),
            pltpu.VMEM((GROUP * rows, keys), F32),
            pltpu.VMEM((GROUP * rows, keys), F32),
            pltpu.VMEM((GROUP * rows, keys), BF16),
            pltpu.VMEM((GROUP * rows, keys), BF16),
            pltpu.VMEM((width, width), F32),
        ],
        compiler_params=params(2),
        name="attend_back",
        cost_estimate=pl.CostEstimate(
            flops=40_000_000_000, transcendentals=pairs * HEADS * rows * keys, bytes_accessed=40_000_000
        ),
    )(*grads, query, key0, value0, key1, value1, bias, mixed, total, weight)


def finish_kernel(
    query_grad, key_grad, value_grad, key_more, value_more, own, far, cap,
    grad_own, grad_far, grad_cap, vec, weight,
    in_own, in_far, in_cap, weight_grad, sums, weight_sum,
):
    pair = pl.program_id(0)
    width, part = own.shape[2], own.shape[1]

    @pl.when(pair == 0)
    def _():
        weight_sum[...] = jnp.zeros_like(weight_sum)
        sums[...] = jnp.zeros_like(sums)

    rows = jnp.concatenate([own[0], far[0], cap[0]], axis=0).astype(F32)
    normed, inverse = standardize(rows)
    first = (normed * vec[0:1] + vec[1:2]).astype(BF16)
    query = query_grad[0]
    key = (key_grad[0] + key_more[0].astype(F32)).astype(BF16)
    value = (value_grad[0] + value_more[0].astype(F32)).astype(BF16)
    first_grad = (
        mm_t(query, weight[:, :width])
        + mm_t(key, weight[:, width : 2 * width])
        + mm_t(value, weight[:, 2 * width :])
    )
    weight_sum[:, :width] += t_mm(first, query)
    weight_sum[:, width : 2 * width] += t_mm(first, key)
    weight_sum[:, 2 * width :] += t_mm(first, value)
    through = norm_through(first_grad, normed, inverse, vec[0:1])
    in_own[0] = grad_own[0] + through[:part]
    in_far[0] = (grad_far[0] + through[part : 2 * part]).astype(BF16)
    in_cap[0] = grad_cap[0] + through[2 * part :]
    sums[...] += jnp.concatenate(
        [
            column_sum(first_grad * normed),
            column_sum(first_grad),
            column_sum(query.astype(F32)),
            column_sum(value.astype(F32)),
            jnp.zeros((4, width), F32),
        ],
        axis=0,
    )

    @pl.when(pair == pl.num_programs(0) - 1)
    def _():
        weight_grad[...] = weight_sum[...].astype(BF16)


def finish(query_grad, key_grad, value_grad, key_more, value_more, own, far, cap, grads, vec, weight):
    pairs, rows, width = query_grad.shape
    part, slots = own.shape[1], cap.shape[1]
    block = lambda n: pl.BlockSpec((1, n, width), lambda i: (i, 0, 0))
    fixed = lambda s: pl.BlockSpec(s, lambda i: (0, 0))
    shape = lambda n, t: jax.ShapeDtypeStruct((pairs, n, width), t)
    split = [block(part), block(part), block(slots)]
    return pl.pallas_call(
        finish_kernel,
        grid=(pairs,),
        in_specs=[block(rows)] * 5 + split + split + [whole(vec.shape), whole(weight.shape)],
        out_specs=split + [fixed((width, 3 * width)), fixed((8, width))],
        out_shape=[shape(part, F32), shape(part, BF16), shape(slots, F32)]
        + [jax.ShapeDtypeStruct((width, 3 * width), BF16), jax.ShapeDtypeStruct((8, width), F32)],
        scratch_shapes=[pltpu.VMEM((width, 3 * width), F32)],
        compiler_params=params(1),
        name="finish",
        cost_estimate=pl.CostEstimate(
            flops=12 * pairs * rows * width * width, transcendentals=0, bytes_accessed=30_000_000
        ),
    )(query_grad, key_grad, value_grad, key_more, value_more, own, far, cap, *grads, vec, weight)


def local(
    images,
    captions,
    lengths,
    first_gain,
    first_shift,
    query_key_value,
    query_bias,
    value_bias,
    output_weight,
    output_bias,
    second_gain,
    second_shift,
    vision_up,
    vision_up_bias,
    vision_down,
    vision_down_bias,
    language_up,
    language_up_bias,
    language_down,
    language_down_bias,
    image_cotangent,
    caption_cotangent,
):
    pair_count, part, width = images.shape
    slots = captions.shape[1]
    streams = lax.axis_size("stream")
    stream = lax.axis_index("stream")
    side, core = stream // 2, stream % 2
    half = pair_count // 2
    across = [(i, (i + 2) % streams) for i in range(streams)]
    beside = [(i, i ^ 1) for i in range(streams)]

    def keep(values):
        return lax.dynamic_slice_in_dim(values, side * half, half, 0)

    def swap(values):
        return lax.ppermute(
            lax.dynamic_slice_in_dim(values, (1 - side) * half, half, 0), "stream", across
        )

    caption_rows = -(-2 * slots // 32) * 32

    def caption_block(mine, theirs):
        filler = jnp.zeros((half, caption_rows - 2 * slots, width), mine.dtype)
        return jnp.concatenate([mine, theirs, filler], axis=1)

    own, far = keep(images), swap(images)
    cap = caption_block(keep(captions), swap(captions))
    vec = jnp.stack(
        [
            first_gain,
            first_shift,
            query_bias,
            value_bias,
            output_bias,
            second_gain,
            second_shift,
            vision_down_bias,
            language_down_bias,
        ]
    )
    rows = 2 * part + caption_rows
    place = jnp.arange(2 * rows, dtype=jnp.int32)
    within = place % rows
    slot = within - 2 * part
    from_core = jnp.where(place < rows, core, 1 - core)
    from_side = jnp.where(slot < slots, side, 1 - side)
    index = (2 * from_side + from_core) * slots + slot % slots
    limit = jnp.where(slot < 2 * slots, index, jnp.int32(2**30))
    limit = jnp.where(within < 2 * part, -1, limit)
    bias = jnp.where(limit[None, :] < keep(lengths)[:, None], 0.0, -1e30)[:, None, :]

    query, key0, value0 = project(own, far, cap, vec, query_key_value)
    key1 = lax.ppermute(key0, "stream", beside)
    value1 = lax.ppermute(value0, "stream", beside)
    cot_own, cot_far = keep(image_cotangent), swap(image_cotangent)
    cot_cap = caption_block(keep(caption_cotangent), swap(caption_cotangent))

    mixed, total, mid_own, mid_far, mid_cap, sec_own, sec_far, sec_cap = attend(
        query, key0, value0, key1, value1, bias, own, far, cap, vec, output_weight
    )
    flat = lambda values: values.reshape(-1, width)
    (out_own, out_far), (grad_own, grad_far), vision_up_bias_grad, vision_sums, vision_grad = expert(
        [flat(sec_own), flat(sec_far)],
        [flat(cot_own), flat(cot_far)],
        [flat(mid_own), flat(mid_far)],
        vec,
        vision_up,
        vision_up_bias[None],
        vision_down,
        512,
        48,
        7,
        True,
    )
    (out_cap,), (grad_cap,), language_up_bias_grad, language_sums = expert(
        [flat(sec_cap)],
        [flat(cot_cap)],
        [flat(mid_cap)],
        vec,
        language_up,
        language_up_bias[None],
        language_down,
        512,
        48,
        8,
        False,
    )
    devices = lax.axis_size("pairs") * streams
    position = lax.axis_index("pairs") * streams + stream

    def gather_captions(values):
        tokens = values[:, : 2 * slots].reshape(-1, width)
        extra = -tokens.shape[0] % 64
        tokens = jnp.concatenate([tokens, jnp.zeros((extra, width), tokens.dtype)], axis=0)
        return lax.all_gather(tokens, BOTH, axis=0, tiled=True)

    units = language_up.shape[1] // devices
    language_up_grad, language_down_grad = share_grads(
        gather_captions(sec_cap),
        gather_captions(cot_cap),
        lax.dynamic_slice_in_dim(language_up, position * units, units, 1),
        lax.dynamic_slice_in_dim(language_up_bias, position * units, units, 0)[None],
        lax.dynamic_slice_in_dim(language_down, position * units, units, 0),
    )
    vision_share = lax.psum_scatter(vision_grad, BOTH, scatter_dimension=0, tiled=True).astype(F32)
    vision_up_grad = vision_share[:, :width].T
    vision_down_grad = vision_share[:, width:]

    grads = [v.reshape(half, -1, width) for v in (grad_own, grad_far, grad_cap)]
    query_grad, key_grad0, value_grad0, key_grad1, value_grad1, output_grad, output_sums = attend_back(
        grads, query, key0, value0, key1, value1, bias, mixed, total, output_weight
    )
    key_more = lax.ppermute(key_grad1, "stream", beside)
    value_more = lax.ppermute(value_grad1, "stream", beside)
    in_own, in_far, in_cap, projection_grad, first_sums = finish(
        query_grad, key_grad0, value_grad0, key_more, value_more, own, far, cap, grads, vec, query_key_value
    )
    projection_grad = lax.psum(projection_grad, BOTH).astype(F32)
    output_grad = lax.psum(output_grad, BOTH).astype(F32)
    small = jnp.concatenate(
        [
            first_sums[:4],
            output_sums[:1],
            vision_sums[:3],
            language_sums[:3],
            vision_up_bias_grad.reshape(-1, width),
            language_up_bias_grad.reshape(-1, width),
        ],
        axis=0,
    )
    small = lax.psum(small, BOTH)
    wide = vision_up_bias.shape[0] // width

    def home(mine, theirs, kind):
        theirs = lax.ppermute(theirs, "stream", across).astype(kind)
        base = jnp.zeros((pair_count,) + mine.shape[1:], kind)
        base = lax.dynamic_update_slice_in_dim(base, mine.astype(kind), side * half, 0)
        return lax.dynamic_update_slice_in_dim(base, theirs, (1 - side) * half, 0)

    shaped = lambda values: values.reshape(half, -1, width)
    out_cap = shaped(out_cap)
    return (
        home(shaped(out_own), shaped(out_far), BF16),
        home(out_cap[:, :slots], out_cap[:, slots : 2 * slots], BF16),
        home(in_own, in_far, F32),
        home(in_cap[:, :slots], in_cap[:, slots : 2 * slots], F32),
        small[0],
        small[1],
        projection_grad,
        small[2],
        small[3],
        output_grad,
        small[4],
        small[5] + small[8],
        small[6] + small[9],
        vision_up_grad,
        small[11 : 11 + wide].reshape(-1),
        vision_down_grad,
        small[7],
        language_up_grad,
        small[11 + wide : 11 + 2 * wide].reshape(-1),
        language_down_grad,
        small[10],
    )


def solution(mesh):
    rows = P("pairs", "stream", None)
    return jax.shard_map(
        local,
        mesh=mesh,
        in_specs=(rows, rows, P("pairs")) + (P(),) * 17 + (rows, rows),
        out_specs=(rows,) * 4
        + (P(),) * 9
        + (
            P(None, BOTH),
            P(),
            P(BOTH, None),
            P(),
            P(None, BOTH),
            P(),
            P(BOTH, None),
            P(),
        ),
        check_vma=False,
    )
```

time: 1640 us -> 615 us (0.38)
  blocking collectives: 428 us -> 52.6 us
  waiting for transfers between devices: 687 us -> 342 us
  matrix products: 231 us -> 0 us
  Pallas kernels: 0 us -> 154 us
  local copies, waits for them, and re-layouts: 153 us -> 25.7 us
  other arithmetic: 116 us -> 11.2 us
    reduce_scatter x4 -> x1, waiting for transfers between devices: 567 us -> 132 us  [local(): lax.psum_scatter(vision_grad, BOTH, scatter_dimension=0, tiled=True)]
    unnamed x1 -> x0, blocking collectives: 385 us -> none
    dot_general x24 -> x0, matrix products: 231 us -> none  [the longest x2 40.2 us: expert_pass(): jnp.einsum('rd,fd->rf', cotangent, down_weight, preferred_element_type=jn...]
    pallas_call x0 -> x7, Pallas kernels: none -> 154 us  [the longest x2 58.2 us: expert(): pl.pallas_call(functools.partial(expert_kernel, parts, with_weights, bloc...]
    reshape x11 -> x6, local copies, waits for them, and re-layouts: 56.7 us -> 1.28 us  [the longest x1 0.61 us: local(): small[11 + wide:11 + 2 * wide].reshape(-1)]
    convert_element_type x9 -> x3, other arithmetic: 50.1 us -> 7.55 us  [the longest x1 3.48 us: local(): projection_grad = lax.psum(projection_grad, BOTH).astype(F32)]
    all_gather x1 -> x2, waiting for transfers between devices: 76.4 us -> 116 us  [gather_captions(): return lax.all_gather(tokens, BOTH, axis=0, tiled=True)]
    reduce_sum x11 -> x0, other arithmetic: 38.1 us -> none  [the longest x1 14.9 us: local(): jnp.sum(jnp.exp(scores - row_top), axis=-1, keepdims=True)]
  transfers between devices with their start and end apart: 6 -> 16, of which waited for: 6 -> 10; matrix products, arithmetic and copies ran while one was open for 8% -> 5% of each run, Pallas kernels for 0% -> 7%
where the time goes in v1:
time: 615 us; the launch traced here: 614 us
  waiting for transfers between devices  342 us (56%)
  Pallas kernels  154 us (25%)
  blocking collectives  52.6 us (9%)
  local copies, waits for them, and re-layouts  25.7 us (4%)
  between operations  14.5 us (2%)
  starting transfers between devices  14.4 us (2%)
  other arithmetic  11.2 us (2%)
    reduce_scatter x1, waiting for transfers between devices, local(): lax.psum_scatter(vision_grad, BOTH, scatter_dimension=0, tiled=True)  132 us
    all_gather x2, waiting for transfers between devices, gather_captions(): return lax.all_gather(tokens, BOTH, axis=0, tiled=True)  116 us
    pallas_call x2, Pallas kernels, expert(): pl.pallas_call(functools.partial(expert_kernel, parts, with_weights, bloc...  58.2 us
    psum x1, waiting for transfers between devices, local(): projection_grad = lax.psum(projection_grad, BOTH).astype(F32)  55.8 us
    psum x1, blocking collectives, local(): small = lax.psum(small, BOTH)  52.6 us
    pallas_call x1, Pallas kernels, attend_back(): pl.pallas_call(attend_back_kernel, grid=(pairs, width // span), in_specs=...  36.5 us
    pallas_call x1, Pallas kernels, attend(): pl.pallas_call(attend_kernel, grid=(pairs, width // span), in_specs=[wide...  27.5 us
    ppermute x4, waiting for transfers between devices, home(): theirs = lax.ppermute(theirs, 'stream', across).astype(kind)  17.7 us
  transfers between devices with their start and end apart: 16, of which 10 were waited for; matrix products, arithmetic and copies ran while one was open for 5% of the time, Pallas kernels for 7%

profile of v1, /device:TPU:0, one launch (start us, length us, event | category | flops | bytes accessed | tf_op | source)
XLA Modules:
  0.0 614.3 jit_solution(15545336595525452536)
XLA Ops:
  7.4 2.3 constant_dynamic-slice_fusion.8
  9.7 3.0 collective-permute-start
  12.7 0.1 constant_dynamic-slice_fusion.3
  13.0 2.1 collective-permute-start.6
  15.4 1.3 stack.39.vec.refs_6_.refs_3_
  16.6 13.4 %collective-permute-done.1 = bf16[3,10,768]{2,1,0:T(8,128)(2,1)S(1)} collective-permute-done((bf16[3,10,768]{2,1,0:T(8,128)(2,1)S(1)}, bf16[3,10,768]{2,1,0:T(8,128)(2,1)S(1)}, u32[]{:S(2)}, u32[]{:S(2)}) %collective-permute-start.1) | collective-permute-done | bytes 46112 | tf_op jit(solution)/shard_map/ppermute | solution.py:542
  30.0 0.8 collective-permute-done.6
  30.8 0.8 maximum_maximum_fusion.1
  31.6 0.9 copy-done.27
  32.5 7.9 %project.1 = (bf16[3,320,768]{2,1,0:T(8,128)(2,1)}, bf16[3,320,768]{2,1,0:T(8,128)(2,1)}, bf16[3,320,768]{2,1,0:T(8,128)(2,1)}) custom-call(bf16[3,144,768]{2,1,0:T(8,128)(2,1)} %get-tuple-element.128.own, bf16[3,144,768]{2,1,0:T(8,128)(2,1)} %copy-done.27, bf16[3,32,768]{2,1,0:T(8,128)(2,1)} %get-tuple-element.140.cap, f32[9,768]{1,0:T(8,128)} %stack.39.vec.refs_6_.refs_3_, ...), custom_call_target="tpu_custom_call" | custom-call | flops 3397386240 | bytes 12000000 | tf_op jit(solution)/shard_map/project/pallas_call | solution.py:74
  40.5 0.5 collective-permute-start.3
  41.0 2.2 constant_dynamic-slice_fusion.4
  43.2 1.7 collective-permute-start.4
  45.0 0.7 compare_select_fusion.bias
  45.7 0.5 collective-permute-done.3.value1
  46.2 27.5 %attend.1 = (bf16[3,320,768]{2,1,0:T(8,128)(2,1)}, f32[3,320,128]{2,1,0:T(8,128)}, f32[3,144,768]{2,1,0:T(8,128)}, f32[3,144,768]{2,1,0:T(8,128)}, f32[3,32,768]...) custom-call(bf16[3,320,768]{2,1,0:T(8,128)(2,1)} %get-tuple-element.57.quer, ...), custom_call_target="tpu_custom_call" | custom-call | flops 20000000000 | bytes 20000000 | tf_op jit(solution)/shard_map/attend/pallas_call | solution.py:151
  73.7 10.7 %expert.1 = (bf16[96,768]{1,0:T(8,128)(2,1)}, f32[96,768]{1,0:T(8,128)}, f32[1,3072]{1,0:T(1,128)}, f32[8,768]{1,0:T(8,128)}) custom-call(bf16[96,768]{1,0:T(8,128)(2,1)} %bitcast.24, bf16[96,768]{1,0:T(8,128)(2,1)} %bitcast.23, f32[96,768]{1,0:T(8,128)} %bitcast.25, f32[9,768]{1,0:T(8,128)} %stack.39.vec.refs_6_.refs_3_, bf16[768,3072]{1,0:T(8,128)(2,1)} %refs_4_.1, ...), custom_call_target="tpu_custom_call" | custom-call | flops 1811939328 | bytes 30000000 | tf_op jit(solution)/shard_map/expert/pallas_call | solution.py:269
  84.4 47.5 %expert_weights.1 = (bf16[432,768]{1,0:T(8,128)(2,1)}, bf16[432,768]{1,0:T(8,128)(2,1)}, f32[432,768]{1,0:T(8,128)}, f32[432,768]{1,0:T(8,128)}, f32[1,3072]{1,0...) custom-call(bf16[432,768]{1,0:T(8,128)(2,1)} %bitcast.37, bf16[432,768]{1,0:T(8,128)(2,1)} %bitcast.38, ...), custom_call_target="tpu_custom_call" | custom-call | flops 24461180928 | bytes 30000000 | tf_op jit(solution)/shard_map/expert_weights/pallas_call | solution.py:269
  131.9 36.5 %attend_back.1 = (bf16[3,320,768]{2,1,0:T(8,128)(2,1)}, f32[3,320,768]{2,1,0:T(8,128)}, f32[3,320,768]{2,1,0:T(8,128)}, bf16[3,320,768]{2,1,0:T(8,128)(2,1)}, bf...) custom-call(f32[3,144,768]{2,1,0:T(8,128)} %bitcast.31, f32[3,144,768]{2,1,0:T(8,128)} %bitcast.33, ...), custom_call_target="tpu_custom_call" | custom-call | flops 40000000000 | bytes 40000000 | tf_op jit(solution)/shard_map/attend_back/pallas_call | solution.py:410
  168.4 0.2 collective-permute-start.8
  168.6 0.4 collective-permute-start.9
  169.0 3.1 collective-permute-done.8.key_more
  172.1 2.1 collective-permute-done.9.value_more
  174.2 17.3 %finish.1 = (f32[3,144,768]{2,1,0:T(8,128)}, bf16[3,144,768]{2,1,0:T(8,128)(2,1)}, f32[3,32,768]{2,1,0:T(8,128)}, bf16[768,2304]{1,0:T(8,128)(2,1)}, f32[8,768]{1,0:T(8,128)}) custom-call(bf16[3,320,768]{2,1,0:T(8,128)(2,1)} %get-tuple-element.74.query_grad, f32[3,320,768]{2,1,0:T(8,128)} %get-tuple-element.75.key_grad, ...), custom_call_target="tpu_custom_call" | custom-call | flops 6794772480 | bytes 30000000 | tf_op jit(solution)/shard_map/finish/pallas_call | solution.py:489
  191.6 0.7 concatenate.23
  192.4 0.7 concatenate.21
  193.2 0.5 reduce-scatter.2.cloned.1.call-update
  193.7 1.8 collective-permute-start.5
  195.5 1.3 dynamic-slice_bitcast_fusion.up_bias
  196.9 1.6 constant_dynamic-slice_fusion.down
  198.4 1.8 constant_dynamic-slice_fusion.1.up
  200.4 0.3 collective-permute-start.7
  200.9 0.1 copy-done.16
  201.0 0.5 broadcast.176
  201.5 0.7 reduce.25
  202.3 0.7 reduce.24
  203.0 0.7 slice.79
  203.8 0.3 dynamic_update_slice.26
  204.1 17.6 %collective-permute-done.7 = bf16[3,10,768]{2,0,1:T(4,128)(2,1)S(1)} collective-permute-done((bf16[3,10,768]{2,0,1:T(4,128)(2,1)S(1)}, bf16[3,10,768]{2,0,1:T(4,128)(2,1)S(1)}, u32[]{:S(2)}, u32[]{:S(2)}) %collective-permute-start.7) | collective-permute-done | bytes 46112 | tf_op jit(solution)/shard_map/ppermute | solution.py:661
  221.7 0.3 dynamic_update_slice.27
  222.2 1.8 collective-permute-start.10
  224.0 0.2 concatenate.20
  224.1 52.6 %psum.21 = f32[19,768]{1,0:T(8,128)S(1)} all-reduce(f32[19,768]{1,0:T(8,128)S(1)} %concatenate.20), channel_id=1, replica_groups=mesh['pairs'=8,'stream'=4] {'pairs','stream'}, use_global_device_ids=true, to_apply=%region_0.1 | all-reduce | flops 14592 | bytes 116736 | tf_op jit(solution)/shard_map/psum | solution.py:657
  276.8 0.6 reshape.198
  277.4 0.6 reshape.195
  278.1 2.3 collective-permute-start.11
  280.5 0.3 dynamic_update_slice.30
  280.8 0.7 copy-done.8
  281.5 0.2 broadcast_in_dim.66
  281.7 1.1 copy-done.3
  282.9 0.7 slice_reduce_fusion
  283.7 1.0 copy.50
  284.6 1.7 dynamic_update_slice.31
  286.5 55.8 %all-reduce.5.cloned.1.call-done = (bf16[768,2304]{1,0:T(8,128)(2,1)}, bf16[768,768]{1,0:T(8,128)(2,1)}) async-done(((bf16[768,2304]{1,0:T(8,128)(2,1)}, bf16[768,768]{1,0:T(8,128)(2,1)}), (bf16[768,2304]{1,0:T(8,128)(2,1)}, bf16[768,768]{1,0:T(8,128)(2,1)})) %all-reduce.5.cloned.1.call-update) | async-done | bytes 4718608 | tf_op jit(solution)/shard_map/psum | solution.py:644
  342.3 3.0 convert_element_type.14
  345.3 3.5 convert_element_type.13
  348.8 54.4 %all-gather.5.cloned.1.call-done.cotangent = bf16[2048,768]{1,0:T(8,128)(2,1)} async-done(((bf16[64,768]{1,0:T(8,128)(2,1)}), bf16[2048,768]{1,0:T(8,128)(2,1)}) %all-gather.5.cloned.1.call-update) | async-done | bytes 3145744 | tf_op jit(solution)/shard_map/all_gather | solution.py:621
  403.2 61.4 %all-gather.3.cloned.1.call-done.second = bf16[2048,768]{1,0:T(8,128)(2,1)} async-done(((bf16[64,768]{1,0:T(8,128)(2,1)}), bf16[2048,768]{1,0:T(8,128)(2,1)}) %all-gather.3.cloned.1.call-update) | async-done | bytes 3145744 | tf_op jit(solution)/shard_map/all_gather | solution.py:621
  464.6 6.5 %share_grads.1 = (f32[768,96]{1,0:T(8,128)}, f32[96,768]{1,0:T(8,128)}) custom-call(bf16[2048,768]{1,0:T(8,128)(2,1)} %all-gather.3.cloned.1.call-done.second, bf16[2048,768]{1,0:T(8,128)(2,1)} %all-gather.5.cloned.1.call-done.cotangent, bf16[768,96]{1,0:T(8,128)(2,1)} %constant_dynamic-slice_fusion.1.up, f32[1,96]{1,0:T(1,128)} %dynamic-slice_bitcast_fusion.up_bias, ...), custom_call_target="tpu_custom_call" | custom-call | flops 1610612736 | bytes 7000000 | tf_op jit(solution)/shard_map/share_grads/pallas_call | solution.py:324
  471.0 1.9 copy.51
  472.9 132.3 %reduce-scatter.2.cloned.1.call-done = bf16[96,1536]{1,0:T(8,128)(2,1)} async-done(((bf16[3072,1536]{1,0:T(8,128)(2,1)}), bf16[96,1536]{1,0:T(8,128)(2,1)}) %reduce-scatter.2.cloned.1.call-update) | async-done | bytes 294928 | tf_op jit(solution)/shard_map/reduce_scatter | solution.py:631
  605.3 1.1 convert_element_type.15
  606.3 0.7 slice_bitcast_fusion
  607.1 0.7 slice.111
  (108 shorter events, 1.6 us)
Async XLA Ops:
  7.2 5.5 copy-start.11
  7.2 5.5 copy-start.12
  7.2 335.1 %all-reduce.5.cloned.1.call-start = ((), (), s32[]{:S(2)}) async-start(), calls=%async_computation.4 | async-start | bytes 9437184 | tf_op jit(solution)/shard_map/psum | solution.py:644
  7.3 7.8 %copy-start.18 = (f32[768]{0:T(1024)S(1)}, f32[768]{0:T(1024)}, u32[]{:S(2)}) copy-start(f32[768]{0:T(1024)} %param.25) | copy-start | bytes 9220
  7.3 7.8 %copy-start.19 = (f32[768]{0:T(1024)S(1)}, f32[768]{0:T(1024)}, u32[]{:S(2)}) copy-start(f32[768]{0:T(1024)} %param.26) | copy-start | bytes 9220
  7.3 7.8 %copy-start.20 = (f32[768]{0:T(1024)S(1)}, f32[768]{0:T(1024)}, u32[]{:S(2)}) copy-start(f32[768]{0:T(1024)} %param.28) | copy-start | bytes 9220
  7.3 7.8 %copy-start.21 = (f32[768]{0:T(1024)S(1)}, f32[768]{0:T(1024)}, u32[]{:S(2)}) copy-start(f32[768]{0:T(1024)} %param.29) | copy-start | bytes 9220
  7.3 7.8 %copy-start.22 = (f32[768]{0:T(1024)S(1)}, f32[768]{0:T(1024)}, u32[]{:S(2)}) copy-start(f32[768]{0:T(1024)} %param.31) | copy-start | bytes 9220
  7.3 7.8 %copy-start.23 = (f32[768]{0:T(1024)S(1)}, f32[768]{0:T(1024)}, u32[]{:S(2)}) copy-start(f32[768]{0:T(1024)} %param.32) | copy-start | bytes 9220
  7.3 7.8 %copy-start.24 = (f32[768]{0:T(1024)S(1)}, f32[768]{0:T(1024)}, u32[]{:S(2)}) copy-start(f32[768]{0:T(1024)} %param.33) | copy-start | bytes 9220
  7.4 7.8 %copy-start.25 = (f32[768]{0:T(1024)S(1)}, f32[768]{0:T(1024)}, u32[]{:S(2)}) copy-start(f32[768]{0:T(1024)} %param.37) | copy-start | bytes 9220
  7.4 7.8 %copy-start.26 = (f32[768]{0:T(1024)S(1)}, f32[768]{0:T(1024)}, u32[]{:S(2)}) copy-start(f32[768]{0:T(1024)} %param.41) | copy-start | bytes 9220
  9.7 21.9 %collective-permute-start = (bf16[3,144,768]{2,1,0:T(8,128)(2,1)S(1)}, bf16[3,144,768]{2,1,0:T(8,128)(2,1)S(1)}, u32[]{:S(2)}, u32[]{:S(2)}) collective-permute-start(bf16[3,144,768]{2,1,0:T(8,128)(2,1)S(1)} %get-tuple-element.127), channel_id=1, source_target_pairs={{0,2},{1,3},{2,0},{3,1},{4,6},{5,7},{6,4},{7,5},{8,10},{9,11},{10,... | collective-permute-start | bytes 1990664 | tf_op jit(solution)/shard_map/ppermute | solution.py:542
  12.9 17.1 %collective-permute-start.1 = (bf16[3,10,768]{2,1,0:T(8,128)(2,1)S(1)}, bf16[3,10,768]{2,1,0:T(8,128)(2,1)S(1)}, u32[]{:S(2)}, u32[]{:S(2)}) collective-permute-start(bf16[3,10,768]{2,1,0:T(8,128)(2,1)S(1)} %copy.53), channel_id=1, source_target_pairs={{0,2},{1,3},{2,0},{3,1},{4,6},{5,7},{6,4},{7,5},{8,10},{9,11},{10,... | collective-permute-start | bytes 138248 | tf_op jit(solution)/shard_map/ppermute | solution.py:542
  13.0 17.8 %collective-permute-start.6 = (bf16[3,10,768]{2,1,0:T(8,128)(2,1)S(1)}, bf16[3,10,768]{2,1,0:T(8,128)(2,1)S(1)}, u32[]{:S(2)}, u32[]{:S(2)}) collective-permute-start(bf16[3,10,768]{2,1,0:T(8,128)(2,1)S(1)} %copy.55), channel_id=1, source_target_pairs={{0,2},{1,3},{2,0},{3,1},{4,6},{5,7},{6,4},{7,5},{8,10},{9,11},{10,... | collective-permute-start | bytes 138248 | tf_op jit(solution)/shard_map/ppermute | solution.py:542
  31.6 0.9 copy-start.27
  40.4 4.6 copy-start.28
  40.4 5.3 collective-permute-start.2
  40.5 5.7 collective-permute-start.3
  43.2 41.2 %collective-permute-start.4 = (bf16[3,144,768]{2,1,0:T(8,128)(2,1)S(1)}, bf16[3,144,768]{2,1,0:T(8,128)(2,1)}, u32[]{:S(2)}, u32[]{:S(2)}) collective-permute-start(bf16[3,144,768]{2,1,0:T(8,128)(2,1)S(1)} %get-tuple-element.125), channel_id=1, source_target_pairs={{0,2},{1,3},{2,0},{3,1},{4,6},{5,7},{6,4},{7,5},{8,10},{9,11},{10,... | collective-permute-start | bytes 1990664 | tf_op jit(solution)/shard_map/ppermute | solution.py:542
  168.4 3.7 collective-permute-start.8
  168.6 5.6 collective-permute-start.9
  191.5 0.9 copy-start.6
  191.5 211.6 %all-gather.5.cloned.1.call-start = ((), (), s32[]{:S(2)}) async-start(), calls=%async_computation.3 | async-start | bytes 3244032 | tf_op jit(solution)/shard_map/all_gather | solution.py:621
  192.3 272.3 %all-gather.3.cloned.1.call-start = ((), (), s32[]{:S(2)}) async-start(), calls=%async_computation.2 | async-start | bytes 3244032 | tf_op jit(solution)/shard_map/all_gather | solution.py:621
  193.1 412.1 %reduce-scatter.2.cloned.1.call-start = ((), (), s32[]{:S(2)}) async-start(), calls=%async_computation.1 | async-start | bytes 9732096 | tf_op jit(solution)/shard_map/reduce_scatter | solution.py:631
  193.2 7.1 %copy-start.9 = (bf16[96,768]{1,0:T(8,128)(2,1)S(1)}, bf16[96,768]{1,0:T(8,128)(2,1)}, u32[]{:S(2)}) copy-start(bf16[96,768]{1,0:T(8,128)(2,1)} %get-tuple-element.68) | copy-start | bytes 442372
  193.7 7.1 %copy-start.5 = (bf16[432,768]{1,0:T(8,128)(2,1)S(1)}, bf16[432,768]{1,0:T(8,128)(2,1)}, u32[]{:S(2)}) copy-start(bf16[432,768]{1,0:T(8,128)(2,1)} %get-tuple-element.64) | copy-start | bytes 1990660
  193.7 28.3 %collective-permute-start.5 = (bf16[3,144,768]{2,1,0:T(8,128)(2,1)}, bf16[3,144,768]{2,1,0:T(8,128)(2,1)S(1)}, u32[]{:S(2)}, u32[]{:S(2)}) collective-permute-start(bf16[3,144,768]{2,1,0:T(8,128)(2,1)} %bitcast.8), channel_id=1, source_target_pairs={{0,2},{1,3},{2,0},{3,1},{4,6},{5,7},{6,4},{7,5},{8,10},{9,11},{10,... | collective-permute-start | bytes 1990664 | tf_op jit(solution)/shard_map/ppermute | solution.py:661
  200.3 0.7 copy-start.16
  200.3 1.2 copy-start.13
  200.3 2.0 copy-start.14
  200.4 2.6 copy-start.15
  200.4 21.3 %collective-permute-start.7 = (bf16[3,10,768]{2,0,1:T(4,128)(2,1)S(1)}, bf16[3,10,768]{2,0,1:T(4,128)(2,1)S(1)}, u32[]{:S(2)}, u32[]{:S(2)}) collective-permute-start(bf16[3,10,768]{2,0,1:T(4,128)(2,1)S(1)} %copy.57), channel_id=1, source_target_pairs={{0,2},{1,3},{2,0},{3,1},{4,6},{5,7},{6,4},{7,5},{8,10},{9,11},{10,... | collective-permute-start | bytes 138248 | tf_op jit(solution)/shard_map/ppermute | solution.py:661
  200.8 21.3 %copy-start.17 = (f32[8,768]{1,0:T(8,128)S(1)}, f32[8,768]{1,0:T(8,128)}, u32[]{:S(2)}) copy-start(f32[8,768]{1,0:T(8,128)} %get-tuple-element.82) | copy-start | bytes 73732
  200.9 77.1 %copy-start.7 = (f32[3,32,768]{2,1,0:T(8,128)S(1)}, f32[3,32,768]{2,1,0:T(8,128)}, u32[]{:S(2)}) copy-start(f32[3,32,768]{2,1,0:T(8,128)} %get-tuple-element.81) | copy-start | bytes 884740
  222.0 56.1 %copy-start.10 = (bf16[6,10,768]{2,0,1:T(8,128)(2,1)}, bf16[6,10,768]{2,0,1:T(8,128)(2,1)S(1)}, u32[]{:S(2)}) copy-start(bf16[6,10,768]{2,0,1:T(8,128)(2,1)S(1)} %dynamic_update_slice.27) | copy-start | bytes 276484
  222.1 58.7 %copy-start.2 = (bf16[6,144,768]{2,1,0:T(8,128)(2,1)}, bf16[6,144,768]{2,1,0:T(8,128)(2,1)S(1)}, u32[]{:S(2)}) copy-start(bf16[6,144,768]{2,1,0:T(8,128)(2,1)S(1)} %constant_dynamic-update-slice_fusion.1) | copy-start | bytes 3981316
  222.2 64.2 %collective-permute-start.10 = (bf16[3,144,768]{2,1,0:T(8,128)(2,1)}, bf16[3,144,768]{2,1,0:T(8,128)(2,1)S(1)}, u32[]{:S(2)}, u32[]{:S(2)}) collective-permute-start(bf16[3,144,768]{2,1,0:T(8,128)(2,1)} %get-tuple-element.80), channel_id=1, source_target_pairs={{0,2},{1,3},{2,0},{3,1},{4,6},{5,7},{6,4},{7,5},{8,10},{9,11},{10,... | collective-permute-start | bytes 1990664 | tf_op jit(solution)/shard_map/ppermute | solution.py:661
  278.1 5.6 collective-permute-start.11
  280.8 0.7 copy-start.8
  281.5 1.3 copy-start.3
  286.5 58.8 %copy-start.1 = (f32[6,144,768]{2,1,0:T(8,128)}, f32[6,144,768]{2,1,0:T(8,128)S(1)}, u32[]{:S(2)}) copy-start(f32[6,144,768]{2,1,0:T(8,128)S(1)} %convert_dynamic-update-slice_fusion) | copy-start | bytes 7962628
  342.3 3.0 copy-start
  605.3 1.8 copy-start.4
Sparse Core Ops, SparseCore 0:
  191.6 150.6 all-reduce.4
  345.2 57.9 all-gather.4
  406.6 57.8 all-gather.2
  470.3 134.8 reduce-scatter.1
